TPU v7x, 32 devices: a whole 2x2x4 slice. The times are simulated.
32 devices in a mesh: frame: 4 (over z), row: 8 (over y, x, core).
Axes of the slice: x: 2, y: 2, z: 4, core: 2. Of those that a mesh axis runs over, the one named last changes fastest.
Arguments:
- fine: bfloat16 [8, 320, 32, 128], P('frame', None, 'row'), may hold values from -6 to 6
- coarse: bfloat16 [4, 64, 1280], P(None, 'row', 'frame'), may hold values from -6 to 6
- w_qkv: bfloat16 [3, 1280, 1280], P(None, None, 'frame'), may hold values from -0.15625 to 0.15625
- w_out: bfloat16 [1280, 1280], P('frame'), may hold values from -0.15625 to 0.15625
- w_up: bfloat16 [1280, 320], P('frame'), may hold values from -0.15625 to 0.15625
- gain_one: float32 [320], replicated, may hold values from 0.1 to 1.9
- conv_space: bfloat16 [3, 3, 320, 320], replicated, may hold values from -0.109375 to 0.109375
- gain_two: float32 [320], replicated, may hold values from 0.1 to 1.9
- conv_time: bfloat16 [3, 320, 320], replicated, may hold values from -0.1875 to 0.1875
Outputs:
- result: bfloat16 [8, 320, 32, 128], P('frame', None, 'row')
All inputs are finite; a program needn't handle non-finite values.
Results may differ from a plain program's by a relative error of at most 0.013.
Values may be sent and summed in bfloat16 or wider, within the bound.
A program may use at most 64 MiB of HBM per device.

v0:
```python
import math
import jax
import jax.numpy as jnp
from jax import lax
from jax.sharding import PartitionSpec as P

HD = 80


def from_partner(value, axis, apart):
    mask = 2**apart
    pairs = [(source, source ^ mask) for source in range(lax.axis_size(axis))]
    return lax.ppermute(value, axis, pairs)


def with_halo(cells, sides, width):
    for axis, dim in sides:
        count = lax.axis_size(axis)
        ends = count - 1
        head = lax.slice_in_dim(cells, 0, width, axis=dim)
        tail = lax.slice_in_dim(cells, cells.shape[dim] - width, cells.shape[dim], axis=dim)
        cells = jnp.concatenate(
            [
                lax.ppermute(tail, axis, [(i, (i + 1) % count) for i in range(ends)]),
                cells,
                lax.ppermute(head, axis, [((i + 1) % count, i) for i in range(ends)]),
            ],
            axis=dim,
        )
    return cells


def norm_silu(values, gain):
    square = jnp.mean(values * values, axis=1, keepdims=True)
    scaled = values * lax.rsqrt(square + 1e-06) * gain[None, :, None, None]
    return jax.nn.silu(scaled).astype(jnp.bfloat16)


def convolve_space(extended, conv_space):
    padded = jnp.pad(extended, ((0, 0), (0, 0), (0, 0), (1, 1)))
    rows_here = extended.shape[2] - 2
    width = extended.shape[3]
    spatial = None
    for offset_y in range(3):
        for offset_x in range(3):
            window = padded[:, :, offset_y : offset_y + rows_here, offset_x : offset_x + width]
            term = jnp.einsum(
                "fcrw,cd->fdrw",
                window,
                conv_space[offset_y, offset_x],
                preferred_element_type=jnp.float32,
            )
            spatial = term if spatial is None else spatial + term
    return spatial


def local(fine, coarse, w_qkv, w_out, w_up, gain_one, conv_space, gain_two, conv_time):
    frame_count = lax.axis_size("frame")
    f_dev = fine.shape[0]
    width = fine.shape[3]
    cf_count, p_dev, c_dev = coarse.shape
    heads_local = w_qkv.shape[2] // HD
    qkv = jnp.einsum(
        "fpc,icd->ifpd",
        lax.all_gather(coarse, "frame", axis=2, tiled=True),
        w_qkv,
        preferred_element_type=jnp.float32,
    ).astype(jnp.bfloat16)
    query = qkv[0].reshape(cf_count, p_dev, heads_local, HD)
    keys = qkv[1].reshape(cf_count, p_dev, heads_local, HD)
    values = qkv[2].reshape(cf_count, p_dev, heads_local, HD)
    scores = jnp.einsum(
        "fphd,gphd->phfg", query, keys, preferred_element_type=jnp.float32
    ) / math.sqrt(HD)
    probs = jax.nn.softmax(scores, axis=-1).astype(jnp.bfloat16)
    attn = jnp.einsum("phfg,gphd->fphd", probs, values, preferred_element_type=jnp.float32).astype(
        jnp.bfloat16
    )
    attn = attn.reshape(cf_count * p_dev, heads_local * HD)
    partial_out = jnp.dot(attn, w_out, preferred_element_type=jnp.float32).reshape(
        cf_count, p_dev, -1
    )
    share = lax.psum_scatter(partial_out, "frame", scatter_dimension=2, tiled=True)
    coarse_out = (coarse.astype(jnp.float32) + share).astype(jnp.bfloat16)
    up_partial = jnp.einsum("fpc,cd->fpd", coarse_out, w_up, preferred_element_type=jnp.float32)
    up_cells = lax.psum(up_partial, "frame").astype(jnp.bfloat16)
    partner = from_partner(up_cells, "row", 0)
    is_even = lax.axis_index("row") % 2 == 0
    coarse_row = jnp.where(
        is_even,
        jnp.concatenate([up_cells, partner], axis=1),
        jnp.concatenate([partner, up_cells], axis=1),
    )
    global_frames = lax.axis_index("frame") * f_dev + jnp.arange(f_dev, dtype=jnp.int32)
    target = global_frames * cf_count // (f_dev * frame_count)
    select = (target[:, None] == jnp.arange(cf_count, dtype=jnp.int32)[None, :]).astype(jnp.float32)
    picked = jnp.einsum("tk,kwc->tcw", select, coarse_row.astype(jnp.float32))
    widened = jnp.repeat(picked, width // picked.shape[2], axis=2)
    merged = (fine.astype(jnp.float32) + widened[:, :, None, :]).astype(jnp.bfloat16)
    first = norm_silu(merged.astype(jnp.float32), gain_one)
    extended = with_halo(first, (("row", 2),), 1)
    second = norm_silu(convolve_space(extended, conv_space), gain_two)
    second_ext = with_halo(second, (("frame", 0),), 1)
    temporal = None
    for offset in range(3):
        term = jnp.einsum(
            "fcrw,cd->fdrw",
            second_ext[offset : offset + f_dev],
            conv_time[offset],
            preferred_element_type=jnp.float32,
        )
        temporal = term if temporal is None else temporal + term
    return (merged.astype(jnp.float32) + temporal).astype(jnp.bfloat16)


def solution(mesh):
    return jax.shard_map(
        local,
        mesh=mesh,
        in_specs=(
            P("frame", None, "row", None),
            P(None, "row", "frame"),
            P(None, None, "frame"),
            P("frame", None),
            P("frame", None),
            P(),
            P(),
            P(),
            P(),
        ),
        out_specs=P("frame", None, "row", None),
        check_vma=False,
    )
```

profile of v0, /device:TPU:12, one launch (start us, length us, event | category | flops | bytes accessed | tf_op | source)
XLA Modules:
  0.0 132.2 jit_solution(14206423180547574291)
XLA Ops:
  6.5 1.1 copy.53
  7.6 25.8 %all_gather.3 = bf16[4,8,1280]{1,0,2:T(4,128)(2,1)} all-gather(bf16[4,8,320]{1,0,2:T(4,128)(2,1)S(1)} %copy.53), channel_id=1, replica_groups=mesh['frame'=4,'row'=8] {'frame'}, dimensions={2}, use_global_device_ids=true | all-gather | bytes 102400 | tf_op jit(solution)/shard_map/all_gather | solution.py:65
  33.5 1.7 %copy.54 = bf16[4,8,1280]{2,1,0:T(8,128)(2,1)S(1)} copy(bf16[4,8,1280]{1,0,2:T(4,128)(2,1)} %all_gather.3) | data formatting | bytes 163840 | tf_op jit(solution)/shard_map/all_gather | solution.py:65
  35.1 0.8 fusion.34
  37.0 1.4 %fusion.39 = f32[4,8,1280]{2,1,0:T(8,128)S(1)} fusion(bf16[4,8,320]{2,1,0:T(8,128)(2,1)S(1)} %dot_general.59, bf16[320,1280]{1,0:T(8,128)(2,1)} %param.12), kind=kOutput, calls=%fused_computation.50 | convolution fusion | flops 26214400 | bytes 1003520 | tf_op jit(solution)/shard_map/dot_general | solution.py:80
  38.4 1.9 %copy.90 = f32[4,8,1280]{1,0,2:T(4,128)} copy(f32[4,8,1280]{2,1,0:T(8,128)S(1)} %fusion.39) | data formatting | bytes 327680
  40.4 3.3 %reshape.62 = f32[1280,32]{1,0:T(8,128)} reshape(f32[1280,4,8]{2,1,0:T(4,128)} %bitcast.157) | data formatting | bytes 327680
  43.7 21.6 %reduce-scatter.4.cloned.1.call-done = f32[320,32]{1,0:T(8,128)} async-done(((f32[1280,32]{1,0:T(8,128)}), f32[320,32]{1,0:T(8,128)}) %reduce-scatter.4.cloned.1.call-update) | async-done | bytes 40976
  65.3 2.1 %reshape.63 = f32[320,4,8]{2,1,0:T(4,128)} reshape(f32[320,32]{1,0:T(8,128)} %reduce-scatter.4.cloned.1.call-done) | data formatting | bytes 81920
  67.4 1.4 %copy.91 = f32[4,8,320]{2,1,0:T(8,128)S(1)} copy(f32[4,8,320]{1,0,2:T(4,128)} %bitcast.158) | data formatting | bytes 81920
  69.0 17.1 %psum.7 = bf16[4,8,320]{2,1,0:T(8,128)(2,1)S(1)} all-reduce(f32[4,8,320]{2,1,0:T(8,128)S(1)} %fusion.72), channel_id=1, replica_groups=mesh['frame'=4,'row'=8] {'frame'}, use_global_device_ids=true, to_apply=%region_3.0 | all-reduce | flops 10240 | bytes 61440 | tf_op jit(solution)/shard_map/psum | solution.py:86
  86.2 1.2 collective-permute-done
  87.6 0.8 broadcast_bitcast_fusion
  88.4 1.2 copy.62
  90.2 2.2 %collective-permute-start.1 = (bf16[2,320,1,128]{3,1,2,0:T(8,128)(2,1)S(1)}, bf16[2,320,1,128]{3,1,2,0:T(8,128)(2,1)S(1)}, u32[]{:S(2)}, u32[]{:S(2)}) collective-permute-start(bf16[2,320,1,128]{3,1,2,0:T(8,128)(2,1)S(1)} %get-tuple-element.7), channel_id=1, source_target_pairs={{0,1},{1,2},{2,3},{3,4},{4,5},{5,6},{6,7},{8,9},{9,10},{10,11},{11... | collective-permute-start | bytes 491528 | tf_op jit(solution)/shard_map/ppermute | solution.py:24
  92.4 4.4 %collective-permute-start.2 = (bf16[2,320,1,128]{3,1,2,0:T(8,128)(2,1)S(1)}, bf16[2,320,1,128]{3,1,2,0:T(8,128)(2,1)S(1)}, u32[]{:S(2)}, u32[]{:S(2)}) collective-permute-start(bf16[2,320,1,128]{3,1,2,0:T(8,128)(2,1)S(1)} %get-tuple-element.8), channel_id=1, source_target_pairs={{1,0},{2,1},{3,2},{4,3},{5,4},{6,5},{7,6},{9,8},{10,9},{11,10},{12... | collective-permute-start | bytes 491528 | tf_op jit(solution)/shard_map/ppermute | solution.py:26
  97.4 0.5 collective-permute-done.1
  97.9 1.8 %collective-permute-done.2 = bf16[2,320,1,128]{3,1,2,0:T(8,128)(2,1)S(1)} collective-permute-done((bf16[2,320,1,128]{3,1,2,0:T(8,128)(2,1)S(1)}, bf16[2,320,1,128]{3,1,2,0:T(8,128)(2,1)S(1)}, u32[]{:S(2)}, u32[]{:S(2)}) %collective-permute-start.2) | collective-permute-done | bytes 163872 | tf_op jit(solution)/shard_map/ppermute | solution.py:26
  99.6 1.0 fusion.8
  101.2 0.7 fusion.53
  101.8 0.7 fusion.44
  103.0 0.5 fusion.55
  103.6 0.6 fusion.16
  104.7 1.0 multiply_reduce_fusion
  106.2 5.0 %collective-permute-start.4 = (bf16[1,320,4,128]{3,1,2,0:T(8,128)(2,1)S(1)}, bf16[1,320,4,128]{3,1,2,0:T(8,128)(2,1)S(1)}, u32[]{:S(2)}, u32[]{:S(2)}) collective-permute-start(bf16[1,320,4,128]{3,1,2,0:T(8,128)(2,1)S(1)} %get-tuple-element.6), channel_id=1, source_target_pairs={{8,0},{16,8},{24,16},{9,1},{17,9},{25,17},{10,2},{18,10},{26,18},{... | collective-permute-start | bytes 983048 | tf_op jit(solution)/shard_map/ppermute | solution.py:26
  111.2 1.9 %collective-permute-start.3 = (bf16[1,320,4,128]{3,1,2,0:T(8,128)(2,1)S(1)}, bf16[1,320,4,128]{3,1,2,0:T(8,128)(2,1)S(1)}, u32[]{:S(2)}, u32[]{:S(2)}) collective-permute-start(bf16[1,320,4,128]{3,1,2,0:T(8,128)(2,1)S(1)} %get-tuple-element.5), channel_id=1, source_target_pairs={{0,8},{8,16},{16,24},{1,9},{9,17},{17,25},{2,10},{10,18},{18,26},{... | collective-permute-start | bytes 983048 | tf_op jit(solution)/shard_map/ppermute | solution.py:24
  113.2 0.5 fusion.59
  113.7 5.5 %collective-permute-done.4 = bf16[1,320,4,128]{3,1,2,0:T(8,128)(2,1)S(1)} collective-permute-done((bf16[1,320,4,128]{3,1,2,0:T(8,128)(2,1)S(1)}, bf16[1,320,4,128]{3,1,2,0:T(8,128)(2,1)S(1)}, u32[]{:S(2)}, u32[]{:S(2)}) %collective-permute-start.4) | collective-permute-done | bytes 327712 | tf_op jit(solution)/shard_map/ppermute | solution.py:26
  119.2 0.5 fusion.41
  119.8 3.6 %collective-permute-done.3 = bf16[1,320,4,128]{3,1,2,0:T(8,128)(2,1)S(1)} collective-permute-done((bf16[1,320,4,128]{3,1,2,0:T(8,128)(2,1)S(1)}, bf16[1,320,4,128]{3,1,2,0:T(8,128)(2,1)S(1)}, u32[]{:S(2)}, u32[]{:S(2)}) %collective-permute-start.3) | collective-permute-done | bytes 327712 | tf_op jit(solution)/shard_map/ppermute | solution.py:24
  123.4 0.6 fusion.17
  124.0 1.3 %copy.75 = bf16[2,320,4,128]{3,2,1,0:T(4,128)(2,1)} copy(bf16[2,320,4,128]{3,1,2,0:T(8,128)(2,1)S(1)} %fusion.17) | data formatting | bytes 1310720 | tf_op jit(solution)/shard_map/convert_element_type | solution.py:113
  (43 shorter events, 4.8 us)
Async XLA Ops:
  6.5 28.6 %copy-start = (bf16[3,1280,320]{1,2,0:T(8,128)(2,1)S(1)}, bf16[3,1280,320]{1,2,0:T(8,128)(2,1)}, u32[]{:S(2)}) copy-start(bf16[3,1280,320]{1,2,0:T(8,128)(2,1)} %param.11) | copy-start | bytes 7372804
  6.5 58.8 %reduce-scatter.4.cloned.1.call-start = ((), (), s32[]{:S(2)}) async-start(), calls=%async_computation.1 | async-start | bytes 819200
  43.7 25.1 %copy-start.4 = (bf16[320,320]{1,0:T(8,128)(2,1)S(1)}, bf16[320,320]{1,0:T(8,128)(2,1)}, u32[]{:S(2)}) copy-start(bf16[320,320]{1,0:T(8,128)(2,1)} %param.13) | copy-start | bytes 614404
  43.7 25.1 %copy-start.5 = (bf16[4,8,320]{2,1,0:T(8,128)(2,1)S(1)}, bf16[4,8,320]{2,1,0:T(8,128)(2,1)}, u32[]{:S(2)}) copy-start(bf16[4,8,320]{2,1,0:T(8,128)(2,1)} %param.10) | copy-start | bytes 61444
  67.4 22.1 %copy-start.1 = (bf16[2,320,4,128]{3,2,1,0:T(4,128)(2,1)S(1)}, bf16[2,320,4,128]{3,2,1,0:T(4,128)(2,1)}, u32[]{:S(2)}) copy-start(bf16[2,320,4,128]{3,2,1,0:T(4,128)(2,1)} %param.9) | copy-start | bytes 1966084
  69.0 20.7 %copy-start.6 = (f32[320]{0:T(512)S(1)}, f32[320]{0:T(512)}, u32[]{:S(2)}) copy-start(f32[320]{0:T(512)} %param.14) | copy-start | bytes 3844
  86.1 1.3 collective-permute-start
  89.7 7.1 %copy-start.2 = (bf16[3,3,320,320]{3,2,1,0:T(8,128)(2,1)S(1)}, bf16[3,3,320,320]{3,2,1,0:T(8,128)(2,1)}, u32[]{:S(2)}) copy-start(bf16[3,3,320,320]{3,2,1,0:T(8,128)(2,1)} %param.15) | copy-start | bytes 5529604
  90.2 7.7 %collective-permute-start.1 = (bf16[2,320,1,128]{3,1,2,0:T(8,128)(2,1)S(1)}, bf16[2,320,1,128]{3,1,2,0:T(8,128)(2,1)S(1)}, u32[]{:S(2)}, u32[]{:S(2)}) collective-permute-start(bf16[2,320,1,128]{3,1,2,0:T(8,128)(2,1)S(1)} %get-tuple-element.7), channel_id=1, source_target_pairs={{0,1},{1,2},{2,3},{3,4},{4,5},{5,6},{6,7},{8,9},{9,10},{10,11},{11... | collective-permute-start | bytes 491528 | tf_op jit(solution)/shard_map/ppermute | solution.py:24
  92.4 7.2 %collective-permute-start.2 = (bf16[2,320,1,128]{3,1,2,0:T(8,128)(2,1)S(1)}, bf16[2,320,1,128]{3,1,2,0:T(8,128)(2,1)S(1)}, u32[]{:S(2)}, u32[]{:S(2)}) collective-permute-start(bf16[2,320,1,128]{3,1,2,0:T(8,128)(2,1)S(1)} %get-tuple-element.8), channel_id=1, source_target_pairs={{1,0},{2,1},{3,2},{4,3},{5,4},{6,5},{7,6},{9,8},{10,9},{11,10},{12... | collective-permute-start | bytes 491528 | tf_op jit(solution)/shard_map/ppermute | solution.py:26
  104.7 1.0 copy-start.7
  105.7 7.5 %copy-start.3 = (bf16[3,320,320]{2,1,0:T(8,128)(2,1)S(1)}, bf16[3,320,320]{2,1,0:T(8,128)(2,1)}, u32[]{:S(2)}) copy-start(bf16[3,320,320]{2,1,0:T(8,128)(2,1)} %param.17) | copy-start | bytes 1843204
  106.2 13.0 %collective-permute-start.4 = (bf16[1,320,4,128]{3,1,2,0:T(8,128)(2,1)S(1)}, bf16[1,320,4,128]{3,1,2,0:T(8,128)(2,1)S(1)}, u32[]{:S(2)}, u32[]{:S(2)}) collective-permute-start(bf16[1,320,4,128]{3,1,2,0:T(8,128)(2,1)S(1)} %get-tuple-element.6), channel_id=1, source_target_pairs={{8,0},{16,8},{24,16},{9,1},{17,9},{25,17},{10,2},{18,10},{26,18},{... | collective-permute-start | bytes 983048 | tf_op jit(solution)/shard_map/ppermute | solution.py:26
  111.2 12.1 %collective-permute-start.3 = (bf16[1,320,4,128]{3,1,2,0:T(8,128)(2,1)S(1)}, bf16[1,320,4,128]{3,1,2,0:T(8,128)(2,1)S(1)}, u32[]{:S(2)}, u32[]{:S(2)}) collective-permute-start(bf16[1,320,4,128]{3,1,2,0:T(8,128)(2,1)S(1)} %get-tuple-element.5), channel_id=1, source_target_pairs={{0,8},{8,16},{16,24},{1,9},{9,17},{17,25},{2,10},{10,18},{18,26},{... | collective-permute-start | bytes 983048 | tf_op jit(solution)/shard_map/ppermute | solution.py:24
Sparse Core Ops, SparseCore 0:
  43.8 21.4 reduce-scatter.3
where the time goes:
time: 133 us; the launch traced here: 132 us
  blocking collectives  42.9 us (32%)
  waiting for transfers between devices  34.2 us (26%)
  local copies, waits for them, and re-layouts  15.2 us (11%)
  between operations  13.7 us (10%)
  starting transfers between devices  13.6 us (10%)
  matrix products  10.4 us (8%)
  other arithmetic  2.09 us (2%)
    all_gather x1, blocking collectives, local(): lax.all_gather(coarse, 'frame', axis=2, tiled=True)  25.8 us
    unnamed x2, waiting for transfers between devices  21.7 us
    psum x1, blocking collectives, local(): up_cells = lax.psum(up_partial, 'frame').astype(jnp.bfloat16)  17.1 us
    unnamed x21, local copies, waits for them, and re-layouts  9.83 us
    ppermute x2, starting transfers between devices, with_halo(): lax.ppermute(head, axis, [((i + 1) % count, i) for i in range(ends)])  9.39 us
    ppermute x2, waiting for transfers between devices, with_halo(): lax.ppermute(head, axis, [((i + 1) % count, i) for i in range(ends)])  7.29 us
    dot_general x9, matrix products, convolve_space(): jnp.einsum('fcrw,cd->fdrw', window, conv_space[offset_y, offset_x], prefe...  5.51 us
    ppermute x2, starting transfers between devices, with_halo(): lax.ppermute(tail, axis, [(i, (i + 1) % count) for i in range(ends)])  4.12 us
  transfers between devices with their start and end apart: 6, of which 6 were waited for; matrix products, arithmetic and copies ran while one was open for 1% of the time, Pallas kernels for 0%

commit v1 on v0

--- a/solution.py
+++ b/solution.py
@@ -5,6 +5,12 @@
 from jax.sharding import PartitionSpec as P
 
 HD = 80
+
+
+def add_all(block, axis):
+    parts = lax.all_gather(block, axis, axis=0, tiled=False)
+    summed = parts.sum(axis=0)
+    return summed
 
 
 def from_partner(value, axis, apart):
@@ -83,7 +89,7 @@
     share = lax.psum_scatter(partial_out, "frame", scatter_dimension=2, tiled=True)
     coarse_out = (coarse.astype(jnp.float32) + share).astype(jnp.bfloat16)
     up_partial = jnp.einsum("fpc,cd->fpd", coarse_out, w_up, preferred_element_type=jnp.float32)
-    up_cells = lax.psum(up_partial, "frame").astype(jnp.bfloat16)
+    up_cells = add_all(up_partial, "frame").astype(jnp.bfloat16)
     partner = from_partner(up_cells, "row", 0)
     is_even = lax.axis_index("row") % 2 == 0
     coarse_row = jnp.where(

time: 133 us -> 127 us (0.955)
  blocking collectives: 42.9 us -> 40.2 us
  local copies, waits for them, and re-layouts: 15.2 us -> 13.2 us
    psum x1 -> x0, blocking collectives: 17.1 us -> none  [local(): up_cells = lax.psum(up_partial, 'frame').astype(jnp.bfloat16)]
    all_gather x0 -> x1, blocking collectives: none -> 14.4 us  [add_all(): parts = lax.all_gather(block, axis, axis=0, tiled=False)]
    unnamed x21, local copies, waits for them, and re-layouts: 9.83 us -> 7.85 us
where the time goes in v1:
time: 127 us
  blocking collectives  40.2 us (32%)
  waiting for transfers between devices  34.2 us (27%)
  between operations  13.7 us (11%)
  local copies, waits for them, and re-layouts  13.2 us (10%)
  starting transfers between devices  12.9 us (10%)
  matrix products  10.4 us (8%)
  other arithmetic  2.11 us (2%)
    all_gather x1, blocking collectives, local(): lax.all_gather(coarse, 'frame', axis=2, tiled=True)  25.8 us
    unnamed x2, waiting for transfers between devices  21.7 us
    all_gather x1, blocking collectives, add_all(): parts = lax.all_gather(block, axis, axis=0, tiled=False)  14.4 us
    ppermute x2, starting transfers between devices, with_halo(): lax.ppermute(head, axis, [((i + 1) % count, i) for i in range(ends)])  8.71 us
    unnamed x21, local copies, waits for them, and re-layouts  7.85 us
    ppermute x2, waiting for transfers between devices, with_halo(): lax.ppermute(head, axis, [((i + 1) % count, i) for i in range(ends)])  7.36 us
    dot_general x9, matrix products, convolve_space(): jnp.einsum('fcrw,cd->fdrw', window, conv_space[offset_y, offset_x], prefe...  5.51 us
    ppermute x2, starting transfers between devices, with_halo(): lax.ppermute(tail, axis, [(i, (i + 1) % count) for i in range(ends)])  4.12 us
  transfers between devices with their start and end apart: 6, of which 6 were waited for; matrix products, arithmetic and copies ran while one was open for 1% of the time, Pallas kernels for 0%

profile of v1, /device:TPU:12, one launch (start us, length us, event | category | flops | bytes accessed | tf_op | source)
XLA Modules:
  0.0 126.8 jit_solution(6504181350930856365)
XLA Ops:
  6.5 1.1 copy.51
  7.6 25.8 %all_gather.9 = bf16[4,8,1280]{1,0,2:T(4,128)(2,1)} all-gather(bf16[4,8,320]{1,0,2:T(4,128)(2,1)S(1)} %copy.51), channel_id=1, replica_groups=mesh['frame'=4,'row'=8] {'frame'}, dimensions={2}, use_global_device_ids=true | all-gather | bytes 102400 | tf_op jit(solution)/shard_map/all_gather | solution.py:71
  33.5 1.7 %copy.52 = bf16[4,8,1280]{2,1,0:T(8,128)(2,1)S(1)} copy(bf16[4,8,1280]{1,0,2:T(4,128)(2,1)} %all_gather.9) | data formatting | bytes 163840 | tf_op jit(solution)/shard_map/all_gather | solution.py:71
  35.1 0.8 fusion.34
  37.0 1.4 %fusion.39 = f32[4,8,1280]{2,1,0:T(8,128)S(1)} fusion(bf16[4,8,320]{2,1,0:T(8,128)(2,1)S(1)} %dot_general.59, bf16[320,1280]{1,0:T(8,128)(2,1)} %param.12), kind=kOutput, calls=%fused_computation.50 | convolution fusion | flops 26214400 | bytes 1003520 | tf_op jit(solution)/shard_map/dot_general | solution.py:86
  38.4 1.9 %copy.88 = f32[4,8,1280]{1,0,2:T(4,128)} copy(f32[4,8,1280]{2,1,0:T(8,128)S(1)} %fusion.39) | data formatting | bytes 327680
  40.4 3.3 %reshape.63 = f32[1280,32]{1,0:T(8,128)} reshape(f32[1280,4,8]{2,1,0:T(4,128)} %bitcast.158) | data formatting | bytes 327680
  43.7 21.6 %reduce-scatter.4.cloned.1.call-done = f32[320,32]{1,0:T(8,128)} async-done(((f32[1280,32]{1,0:T(8,128)}), f32[320,32]{1,0:T(8,128)}) %reduce-scatter.4.cloned.1.call-update) | async-done | bytes 40976
  65.3 1.2 reshape.64
  67.0 14.4 %all-gather = f32[16,8,320]{2,1,0:T(8,128)S(1)} all-gather(f32[4,8,320]{2,1,0:T(8,128)S(1)} %fusion.72), channel_id=2, replica_groups=mesh['frame'=4,'row'=8] {'frame'}, dimensions={0}, use_global_device_ids=true | all-gather | bytes 204800 | tf_op jit(solution)/shard_map/all_gather | solution.py:11
  81.5 1.2 collective-permute-done
  82.9 0.8 broadcast_bitcast_fusion
  83.7 1.2 copy.60
  85.6 2.2 %collective-permute-start.1 = (bf16[2,320,1,128]{3,1,2,0:T(8,128)(2,1)S(1)}, bf16[2,320,1,128]{3,1,2,0:T(8,128)(2,1)S(1)}, u32[]{:S(2)}, u32[]{:S(2)}) collective-permute-start(bf16[2,320,1,128]{3,1,2,0:T(8,128)(2,1)S(1)} %get-tuple-element.7), channel_id=1, source_target_pairs={{0,1},{1,2},{2,3},{3,4},{4,5},{5,6},{6,7},{8,9},{9,10},{10,11},{11... | collective-permute-start | bytes 491528 | tf_op jit(solution)/shard_map/ppermute | solution.py:30
  87.8 4.4 %collective-permute-start.2 = (bf16[2,320,1,128]{3,1,2,0:T(8,128)(2,1)S(1)}, bf16[2,320,1,128]{3,1,2,0:T(8,128)(2,1)S(1)}, u32[]{:S(2)}, u32[]{:S(2)}) collective-permute-start(bf16[2,320,1,128]{3,1,2,0:T(8,128)(2,1)S(1)} %get-tuple-element.8), channel_id=1, source_target_pairs={{1,0},{2,1},{3,2},{4,3},{5,4},{6,5},{7,6},{9,8},{10,9},{11,10},{12... | collective-permute-start | bytes 491528 | tf_op jit(solution)/shard_map/ppermute | solution.py:32
  92.2 0.5 fusion.66
  92.7 0.5 collective-permute-done.1
  93.2 1.8 %collective-permute-done.2 = bf16[2,320,1,128]{3,1,2,0:T(8,128)(2,1)S(1)} collective-permute-done((bf16[2,320,1,128]{3,1,2,0:T(8,128)(2,1)S(1)}, bf16[2,320,1,128]{3,1,2,0:T(8,128)(2,1)S(1)}, u32[]{:S(2)}, u32[]{:S(2)}) %collective-permute-start.2) | collective-permute-done | bytes 163872 | tf_op jit(solution)/shard_map/ppermute | solution.py:32
  95.0 1.0 fusion.8
  96.5 0.7 fusion.53
  97.2 0.7 fusion.44
  98.4 0.5 fusion.55
  98.9 0.6 fusion.16
  100.0 1.0 multiply_reduce_fusion
  101.6 4.3 %collective-permute-start.4 = (bf16[1,320,4,128]{3,1,2,0:T(8,128)(2,1)S(1)}, bf16[1,320,4,128]{3,1,2,0:T(8,128)(2,1)S(1)}, u32[]{:S(2)}, u32[]{:S(2)}) collective-permute-start(bf16[1,320,4,128]{3,1,2,0:T(8,128)(2,1)S(1)} %get-tuple-element.6), channel_id=1, source_target_pairs={{8,0},{16,8},{24,16},{9,1},{17,9},{25,17},{10,2},{18,10},{26,18},{... | collective-permute-start | bytes 983048 | tf_op jit(solution)/shard_map/ppermute | solution.py:32
  105.9 1.9 %collective-permute-start.3 = (bf16[1,320,4,128]{3,1,2,0:T(8,128)(2,1)S(1)}, bf16[1,320,4,128]{3,1,2,0:T(8,128)(2,1)S(1)}, u32[]{:S(2)}, u32[]{:S(2)}) collective-permute-start(bf16[1,320,4,128]{3,1,2,0:T(8,128)(2,1)S(1)} %get-tuple-element.5), channel_id=1, source_target_pairs={{0,8},{8,16},{16,24},{1,9},{9,17},{17,25},{2,10},{10,18},{18,26},{... | collective-permute-start | bytes 983048 | tf_op jit(solution)/shard_map/ppermute | solution.py:30
  107.8 0.5 fusion.59
  108.4 5.6 %collective-permute-done.4 = bf16[1,320,4,128]{3,1,2,0:T(8,128)(2,1)S(1)} collective-permute-done((bf16[1,320,4,128]{3,1,2,0:T(8,128)(2,1)S(1)}, bf16[1,320,4,128]{3,1,2,0:T(8,128)(2,1)S(1)}, u32[]{:S(2)}, u32[]{:S(2)}) %collective-permute-start.4) | collective-permute-done | bytes 327712 | tf_op jit(solution)/shard_map/ppermute | solution.py:32
  114.0 0.5 fusion.41
  114.5 3.5 %collective-permute-done.3 = bf16[1,320,4,128]{3,1,2,0:T(8,128)(2,1)S(1)} collective-permute-done((bf16[1,320,4,128]{3,1,2,0:T(8,128)(2,1)S(1)}, bf16[1,320,4,128]{3,1,2,0:T(8,128)(2,1)S(1)}, u32[]{:S(2)}, u32[]{:S(2)}) %collective-permute-start.3) | collective-permute-done | bytes 327712 | tf_op jit(solution)/shard_map/ppermute | solution.py:30
  118.0 0.6 fusion.17
  118.7 1.3 %copy.73 = bf16[2,320,4,128]{3,2,1,0:T(4,128)(2,1)} copy(bf16[2,320,4,128]{3,1,2,0:T(8,128)(2,1)S(1)} %fusion.17) | data formatting | bytes 1310720 | tf_op jit(solution)/shard_map/convert_element_type | solution.py:119
  (44 shorter events, 4.5 us)
Async XLA Ops:
  6.5 28.6 %copy-start = (bf16[3,1280,320]{1,2,0:T(8,128)(2,1)S(1)}, bf16[3,1280,320]{1,2,0:T(8,128)(2,1)}, u32[]{:S(2)}) copy-start(bf16[3,1280,320]{1,2,0:T(8,128)(2,1)} %param.11) | copy-start | bytes 7372804
  6.5 58.8 %reduce-scatter.4.cloned.1.call-start = ((), (), s32[]{:S(2)}) async-start(), calls=%async_computation.1 | async-start | bytes 819200
  43.7 23.2 %copy-start.4 = (bf16[320,320]{1,0:T(8,128)(2,1)S(1)}, bf16[320,320]{1,0:T(8,128)(2,1)}, u32[]{:S(2)}) copy-start(bf16[320,320]{1,0:T(8,128)(2,1)} %param.13) | copy-start | bytes 614404
  43.7 23.2 %copy-start.5 = (bf16[4,8,320]{2,1,0:T(8,128)(2,1)S(1)}, bf16[4,8,320]{2,1,0:T(8,128)(2,1)}, u32[]{:S(2)}) copy-start(bf16[4,8,320]{2,1,0:T(8,128)(2,1)} %param.10) | copy-start | bytes 61444
  66.8 18.0 %copy-start.1 = (bf16[2,320,4,128]{3,2,1,0:T(4,128)(2,1)S(1)}, bf16[2,320,4,128]{3,2,1,0:T(4,128)(2,1)}, u32[]{:S(2)}) copy-start(bf16[2,320,4,128]{3,2,1,0:T(4,128)(2,1)} %param.9) | copy-start | bytes 1966084
  81.4 3.6 %copy-start.6 = (f32[320]{0:T(512)S(1)}, f32[320]{0:T(512)}, u32[]{:S(2)}) copy-start(f32[320]{0:T(512)} %param.14) | copy-start | bytes 3844
  81.4 1.3 collective-permute-start
  85.0 7.1 %copy-start.2 = (bf16[3,3,320,320]{3,2,1,0:T(8,128)(2,1)S(1)}, bf16[3,3,320,320]{3,2,1,0:T(8,128)(2,1)}, u32[]{:S(2)}) copy-start(bf16[3,3,320,320]{3,2,1,0:T(8,128)(2,1)} %param.15) | copy-start | bytes 5529604
  85.6 7.7 %collective-permute-start.1 = (bf16[2,320,1,128]{3,1,2,0:T(8,128)(2,1)S(1)}, bf16[2,320,1,128]{3,1,2,0:T(8,128)(2,1)S(1)}, u32[]{:S(2)}, u32[]{:S(2)}) collective-permute-start(bf16[2,320,1,128]{3,1,2,0:T(8,128)(2,1)S(1)} %get-tuple-element.7), channel_id=1, source_target_pairs={{0,1},{1,2},{2,3},{3,4},{4,5},{5,6},{6,7},{8,9},{9,10},{10,11},{11... | collective-permute-start | bytes 491528 | tf_op jit(solution)/shard_map/ppermute | solution.py:30
  87.8 7.2 %collective-permute-start.2 = (bf16[2,320,1,128]{3,1,2,0:T(8,128)(2,1)S(1)}, bf16[2,320,1,128]{3,1,2,0:T(8,128)(2,1)S(1)}, u32[]{:S(2)}, u32[]{:S(2)}) collective-permute-start(bf16[2,320,1,128]{3,1,2,0:T(8,128)(2,1)S(1)} %get-tuple-element.8), channel_id=1, source_target_pairs={{1,0},{2,1},{3,2},{4,3},{5,4},{6,5},{7,6},{9,8},{10,9},{11,10},{12... | collective-permute-start | bytes 491528 | tf_op jit(solution)/shard_map/ppermute | solution.py:32
  100.0 1.0 copy-start.7
  101.0 6.8 %copy-start.3 = (bf16[3,320,320]{2,1,0:T(8,128)(2,1)S(1)}, bf16[3,320,320]{2,1,0:T(8,128)(2,1)}, u32[]{:S(2)}) copy-start(bf16[3,320,320]{2,1,0:T(8,128)(2,1)} %param.17) | copy-start | bytes 1843204
  101.6 12.4 %collective-permute-start.4 = (bf16[1,320,4,128]{3,1,2,0:T(8,128)(2,1)S(1)}, bf16[1,320,4,128]{3,1,2,0:T(8,128)(2,1)S(1)}, u32[]{:S(2)}, u32[]{:S(2)}) collective-permute-start(bf16[1,320,4,128]{3,1,2,0:T(8,128)(2,1)S(1)} %get-tuple-element.6), channel_id=1, source_target_pairs={{8,0},{16,8},{24,16},{9,1},{17,9},{25,17},{10,2},{18,10},{26,18},{... | collective-permute-start | bytes 983048 | tf_op jit(solution)/shard_map/ppermute | solution.py:32
  105.9 12.1 %collective-permute-start.3 = (bf16[1,320,4,128]{3,1,2,0:T(8,128)(2,1)S(1)}, bf16[1,320,4,128]{3,1,2,0:T(8,128)(2,1)S(1)}, u32[]{:S(2)}, u32[]{:S(2)}) collective-permute-start(bf16[1,320,4,128]{3,1,2,0:T(8,128)(2,1)S(1)} %get-tuple-element.5), channel_id=1, source_target_pairs={{0,8},{8,16},{16,24},{1,9},{9,17},{17,25},{2,10},{10,18},{18,26},{... | collective-permute-start | bytes 983048 | tf_op jit(solution)/shard_map/ppermute | solution.py:30
Sparse Core Ops, SparseCore 0:
  43.8 21.4 reduce-scatter.3
